TPU v7x, 256 devices: a 8x8x2 block of a 8x8x16 slice. The times are simulated.
256 devices in a mesh: group: 2 (over z), tp: 16 (over x, core), dp: 8 (over y).
Axes of the slice: x: 8, y: 8, z: 2, core: 2. Of those that a mesh axis runs over, the one named last changes fastest.
The devices are a block of a 8x8x16 slice.
Arguments:
- patches: bfloat16 [1024, 128, 1280], P(('group', 'tp', 'dp')), parts along dimension 0, may hold values from -38 to 38, as said below
- patch_counts: int32 [1024], P(('group', 'tp', 'dp')), parts along dimension 0, may hold values from 0 to 128, as said below
- encoder_index: int32 [1024], P(('group', 'tp', 'dp')), parts along dimension 0, may hold values from 0 to 7, as said below
- vit_gain: float32 [1280], replicated, may hold values from 0.1 to 1.9
- vit_up: bfloat16 [1280, 5120], P(None, 'tp'), may hold values from -0.15625 to 0.15625
- vit_down: bfloat16 [5120, 1280], P('tp'), may hold values from -0.078125 to 0.078125
- queries: bfloat16 [64, 32, 128], P(('group', 'dp')), parts along dimension 0, may hold values from -20 to 20
- cache_keys: bfloat16 [64, 4, 8192, 128], P(('group', 'dp'), None, 'tp'), parts along dimension 0, may hold values from -6 to 6
- cache_values: bfloat16 [64, 4, 8192, 128], P(('group', 'dp'), None, 'tp'), parts along dimension 0, may hold values from -6 to 6
- new_keys: bfloat16 [64, 4, 128], P(('group', 'dp')), parts along dimension 0, may hold values from -6 to 6
- new_values: bfloat16 [64, 4, 128], P(('group', 'dp')), parts along dimension 0, may hold values from -6 to 6
- kv_lengths: int32 [64], P(('group', 'dp')), parts along dimension 0, may hold values from 2 to 8192, as said below
- out_weight: bfloat16 [4096, 8192], P(None, 'tp'), may hold values from -0.09375 to 0.09375
Outputs:
- embeddings: bfloat16 [768, 128, 1280], P(('group', 'tp', 'dp')), parts along dimension 0
- decoded: bfloat16 [64, 8192], P(('group', 'dp'), 'tp'), parts along dimension 0
There are 2 independent parts, one for each index of `group`. A program takes and returns all parts, laid end to end along the dimension named above; an argument that names none is the same for every part. Nothing has to cross between parts.
Inputs may be any that keep to these rules, and one draw needn't show every extreme that they name: `patches`: draws of spread scale. `patch_counts`: 0 marks an empty slot. Each device holds between 1 and 4 non-empty slots and some device holds 4; each tp row of 8 devices holds exactly 24 non-empty slots; some slot has 128 patches. `encoder_index`: indices into the dp axis within the slot's own tp row. The non-empty slots of one device name distinct encoders, and every encoder is named by exactly 3 non-empty slots of its tp row. Entries of empty slots carry no meaning. `kv_lengths`: some sequence uses all 8192 positions.
All inputs are finite; a program needn't handle non-finite values.
Results may differ from a plain program's by a relative error of at most 0.015.
Values may be sent and summed in bfloat16 or wider, within the bound.
A program may use at most 192 MiB of HBM per device.

v0:
```python
import jax
import jax.numpy as jnp
from jax import lax
from jax.sharding import PartitionSpec as P

RECV_MAX = 3


def gather_turned(arrays, axis, dims):
    turned = [jnp.moveaxis(a, dim, 0) for a, dim in zip(arrays, dims)]
    widths = [t[0].size for t in turned]
    both = jnp.concatenate([t.reshape(-1, w) for t, w in zip(turned, widths)], axis=1)
    whole = lax.all_gather(both, axis, axis=0, tiled=True)
    blocks = jnp.split(whole, [sum(widths[:k]) for k in range(1, len(widths))], axis=1)
    return tuple(
        (
            jnp.moveaxis(b.reshape(-1, *t.shape[1:]), 0, dim)
            for b, t, dim in zip(blocks, turned, dims)
        )
    )


def from_everyone(array, axis):
    copies = jnp.broadcast_to(array, (lax.axis_size(axis), *array.shape))
    return lax.all_to_all(copies, axis, split_axis=0, concat_axis=0, tiled=True)


def over_copies(array, axis):
    everything = from_everyone(array, axis)
    return jnp.max(everything, axis=0)


def over_pieces(array, axis):
    blocks = lax.all_gather(array, axis).astype(jnp.float32)
    return blocks.sum(axis=0)


def quick_gelu(values):
    return values * jax.nn.sigmoid(1.702 * values)


def vit_block(block_rows, vit_gain, vit_up, vit_down):
    xfloat = block_rows.astype(jnp.float32)
    center = xfloat - jnp.mean(xfloat, axis=-1, keepdims=True)
    spread = jnp.mean(center * center, axis=-1, keepdims=True)
    normed = (center * lax.rsqrt(spread + 1e-06) * vit_gain).astype(jnp.bfloat16)
    up_whole, down_whole = gather_turned((vit_up, vit_down), "tp", (1, 0))
    hidden = quick_gelu(jnp.dot(normed, up_whole, preferred_element_type=jnp.float32)).astype(
        jnp.bfloat16
    )
    branch = jnp.dot(hidden, down_whole, preferred_element_type=jnp.float32)
    return (xfloat + branch).astype(jnp.bfloat16)


def mask_rows(blocks, counts):
    keep = jnp.arange(blocks.shape[1], dtype=jnp.int32)[None, :] < counts[:, None]
    return jnp.where(keep[:, :, None], blocks, jnp.zeros_like(blocks))


def place_images(patches, patch_counts, encoder_index, vit_gain, vit_up, vit_down):
    slot_count, row_count, feature_width = patches.shape
    groups = lax.axis_size("dp")
    live_slots = patch_counts > 0
    targets = (jnp.arange(groups, dtype=jnp.int32)[:, None] == encoder_index[None, :]) & live_slots[
        None, :
    ]
    select = targets.astype(jnp.bfloat16)
    outgoing = jnp.dot(
        select,
        patches.reshape(slot_count, row_count * feature_width),
        preferred_element_type=jnp.float32,
    )
    outgoing = outgoing.astype(jnp.bfloat16).reshape(groups, row_count, feature_width)
    sent_counts = jnp.sum(jnp.where(targets, patch_counts[None, :], 0), axis=1).astype(jnp.bfloat16)
    arrived, arrived_counts = (
        lax.all_to_all(outgoing, "dp", split_axis=0, concat_axis=0, tiled=True),
        lax.all_to_all(sent_counts, "dp", split_axis=0, concat_axis=0, tiled=True),
    )
    present = arrived_counts > 0
    ranking = jnp.cumsum(present.astype(jnp.int32)) - 1
    pick_mask = (jnp.arange(RECV_MAX, dtype=jnp.int32)[:, None] == ranking[None, :]) & present[
        None, :
    ]
    picker = pick_mask.astype(jnp.bfloat16)
    gathered = jnp.dot(
        picker,
        arrived.reshape(groups, row_count * feature_width),
        preferred_element_type=jnp.float32,
    )
    gathered = gathered.astype(jnp.bfloat16).reshape(RECV_MAX, row_count, feature_width)
    kept_counts = jnp.sum(
        jnp.where(pick_mask, arrived_counts.astype(jnp.float32)[None, :], 0.0), axis=1
    ).astype(jnp.int32)
    encoded = vit_block(
        gathered.reshape(RECV_MAX * row_count, feature_width), vit_gain, vit_up, vit_down
    )
    gathered = mask_rows(encoded.reshape(RECV_MAX, row_count, feature_width), kept_counts)
    return gathered


def decode_step(queries, cache_keys, cache_values, new_keys, new_values, kv_lengths, out_weight):
    seq_count, kv_heads, span, head_dim = cache_keys.shape
    per_group = queries.shape[1] // kv_heads
    scale = head_dim ** (-0.5)
    grouped = queries.reshape(seq_count, kv_heads, per_group, head_dim)
    positions = lax.axis_index("tp") * span + jnp.arange(span, dtype=jnp.int32)
    valid = positions[None, :] < kv_lengths[:, None]
    scores = (
        jnp.einsum("skgd,skpd->skgp", grouped, cache_keys, preferred_element_type=jnp.float32)
        * scale
    )
    scores = jnp.where(valid[:, None, None, :], scores, -1e30)
    own = jnp.einsum("skgd,skd->skg", grouped, new_keys, preferred_element_type=jnp.float32) * scale
    local_top = jnp.maximum(jnp.max(scores, axis=-1), own)
    top = over_copies(local_top, "tp")
    weights = jnp.exp(scores - top[..., None])
    local_total = jnp.sum(weights, axis=-1)
    local_mix = jnp.einsum(
        "skgp,skpd->skgd",
        weights.astype(jnp.bfloat16),
        cache_values,
        preferred_element_type=jnp.float32,
    )
    total, mixed = (
        over_pieces(local_total.astype(jnp.bfloat16), "tp").astype(jnp.float32),
        over_pieces(local_mix.astype(jnp.bfloat16), "tp").astype(jnp.float32),
    )
    own_weight = jnp.exp(own - top)
    total = total + own_weight
    own_rounded = lax.optimization_barrier(own_weight.astype(jnp.bfloat16)).astype(jnp.float32)
    mixed = mixed + own_rounded[..., None] * new_values.astype(jnp.float32)[:, :, None, :]
    attended = (mixed / total[..., None]).astype(jnp.bfloat16).reshape(seq_count, -1)
    return jnp.dot(attended, out_weight, preferred_element_type=jnp.float32).astype(jnp.bfloat16)


def local(
    patches,
    patch_counts,
    encoder_index,
    vit_gain,
    vit_up,
    vit_down,
    queries,
    cache_keys,
    cache_values,
    new_keys,
    new_values,
    kv_lengths,
    out_weight,
):
    decoded = decode_step(
        queries, cache_keys, cache_values, new_keys, new_values, kv_lengths, out_weight
    )
    embeddings = place_images(patches, patch_counts, encoder_index, vit_gain, vit_up, vit_down)
    return (embeddings, decoded)


def solution(mesh):
    return jax.shard_map(
        local,
        mesh=mesh,
        in_specs=(
            P(("group", "tp", "dp"), None, None),
            P(("group", "tp", "dp")),
            P(("group", "tp", "dp")),
            P(),
            P(None, "tp"),
            P("tp", None),
            P(("group", "dp"), None, None),
            P(("group", "dp"), None, "tp", None),
            P(("group", "dp"), None, "tp", None),
            P(("group", "dp"), None, None),
            P(("group", "dp"), None, None),
            P(("group", "dp")),
            P(None, "tp"),
        ),
        out_specs=(P(("group", "tp", "dp"), None, None), P(("group", "dp"), "tp")),
        check_vma=False,
    )
```

profile of v0, /device:TPU:513, one launch (start us, length us, event | category | flops | bytes accessed | tf_op | source)
XLA Modules:
  0.0 202.3 jit_solution(7990581057906296930)
XLA Ops:
  7.3 2.8 %pad_maximum_fusion = bf16[320,2560]{1,0:T(8,128)(2,1)} fusion(bf16[320,1280]{1,0:T(8,128)(2,1)} %param.18, bf16[320,1280]{1,0:T(8,128)(2,1)} %bitcast.43), kind=kLoop, calls=%fused_computation.14 | loop fusion | flops 3276800 | bytes 3276800 | tf_op jit(solution)/shard_map/concatenate | solution.py:12
  10.3 0.7 copy.21
  11.0 13.7 %all-to-all-start = ((bf16[8,1,1]{2,1,0:T(2,128)(2,1)}), bf16[8,1,1]{2,1,0:T(2,128)(2,1)S(1)}, u32[]{:S(2)}, u32[]{:S(2)}) async-start(bf16[8,1,1]{2,1,0:T(2,128)(2,1)} %copy.21), calls=%async_computation | async-start | bytes 8192 | tf_op jit(solution)/shard_map/all_to_all | solution.py:77
  24.7 2.3 %copy.27 = bf16[1,4,128,1280]{3,1,2,0:T(4,128)(2,1)S(1)} copy(bf16[1,4,128,1280]{3,2,1,0:T(8,128)(2,1)} %bitcast.41) | data formatting | bytes 2621440
  27.3 1.4 fusion.52
  28.7 0.8 reshape.189
  29.4 1.7 all-to-all-done
  31.2 14.4 %all-to-all-start.2 = ((f32[16,1,128]{2,1,0:T(1,128)}), f32[16,1,128]{2,1,0:T(1,128)S(1)}, u32[]{:S(2)}, u32[]{:S(2)}) async-start(f32[16,1,128]{2,1,0:T(1,128)} %reshape.189), calls=%async_computation.2 | async-start | bytes 16384 | tf_op jit(solution)/shard_map/all_to_all | solution.py:25
  45.6 2.0 %convolution_convert_fusion = bf16[8,163840]{1,0:T(8,128)(2,1)S(1)} fusion(bf16[4,163840]{1,0:T(4,128)(2,1)S(1)} %bitcast.39, s32[4]{0:T(128)S(1)} %copy-done.4, pred[4]{0:T(512)(128)(4,1)} %copy-done.5), kind=kOutput, calls=%fused_computation | convolution fusion | flops 11796544 | bytes 3932180 | tf_op jit(solution)/shard_map/dot_general | solution.py:68
  47.6 2.0 copy.22
  49.6 3.4 %all-to-all-done.2 = f32[16,1,128]{2,1,0:T(1,128)S(1)} async-done(((f32[16,1,128]{2,1,0:T(1,128)}), f32[16,1,128]{2,1,0:T(1,128)S(1)}, u32[]{:S(2)}, u32[]{:S(2)}) %all-to-all-start.2) | async-done | bytes 8224 | tf_op jit(solution)/shard_map/all_to_all | solution.py:25
  53.0 4.6 %all-to-all-start.1 = ((bf16[8,128,1280]{2,1,0:T(8,128)(2,1)}), bf16[8,128,1280]{2,1,0:T(8,128)(2,1)}, u32[]{:S(2)}, u32[]{:S(2)}) async-start(bf16[8,128,1280]{2,1,0:T(8,128)(2,1)} %copy.22), calls=%async_computation.1 | async-start | bytes 5242880 | tf_op jit(solution)/shard_map/all_to_all | solution.py:76
  57.6 0.2 fusion.39
  57.8 0.2 reduce-window.8
  58.2 0.2 compare_reduce_fusion
  58.6 0.5 broadcast.122
  59.2 0.7 reduce.6
  59.8 0.2 reshape.190
  60.1 0.2 fusion.28
  60.3 16.2 %all-gather.1 = bf16[64,4,8]{2,1,0:T(4,128)(2,1)S(1)} all-gather(bf16[4,4,8]{2,1,0:T(4,128)(2,1)S(1)} %fusion.28), channel_id=3, replica_groups=mesh['group'=2,'tp'=16,'dp'=8] {'tp'}, dimensions={0}, use_global_device_ids=true | all-gather | bytes 4352 | tf_op jit(solution)/shard_map/all_gather | solution.py:34
  76.5 2.1 %convolution_convert_fusion.2 = bf16[4,4,8,128]{3,2,1,0:T(8,128)(2,1)S(1)} fusion(bf16[4,4,512,128]{3,2,1,0:T(8,128)(2,1)} %param.21, f32[4,4,8,512]{3,2,1,0:T(8,128)S(1)} %copy-done.1, f32[4,4,8]{2,1,0:T(4,128)S(1)} %reduce_max.19), kind=kOutput, calls=%fused_computation.17 | convolution fusion | flops 16924672 | bytes 2392576 | tf_op jit(solution)/shard_map/skgp,skpd->skgd/dot_general | solution.py:118
  78.6 20.6 %all-gather = bf16[64,4,8,128]{3,2,1,0:T(8,128)(2,1)S(1)} all-gather(bf16[4,4,8,128]{3,2,1,0:T(8,128)(2,1)S(1)} %convolution_convert_fusion.2), channel_id=2, replica_groups=mesh['group'=2,'tp'=16,'dp'=8] {'tp'}, dimensions={0}, use_global_device_ids=true | all-gather | bytes 557056 | tf_op jit(solution)/shard_map/all_gather | solution.py:34
  99.4 3.4 %convolution_convert_fusion.3 = bf16[4,512]{1,0:T(4,128)(2,1)} fusion(bf16[4096,512]{1,0:T(8,128)(2,1)} %param.25, bf16[1,4,32,128]{3,2,1,0:T(8,128)(2,1)S(1)} %fusion.37), kind=kOutput, calls=%fused_computation.18 | convolution fusion | flops 16779264 | bytes 4231168 | tf_op jit(solution)/shard_map/dot_general | solution.py:133
  102.9 17.7 %all-to-all-done.1 = bf16[8,128,1280]{2,1,0:T(8,128)(2,1)} async-done(((bf16[8,128,1280]{2,1,0:T(8,128)(2,1)}), bf16[8,128,1280]{2,1,0:T(8,128)(2,1)}, u32[]{:S(2)}, u32[]{:S(2)}) %all-to-all-start.1) | async-done | bytes 2621472 | tf_op jit(solution)/shard_map/all_to_all | solution.py:76
  120.6 3.2 %copy.28 = bf16[1,8,128,1280]{3,1,2,0:T(8,128)(2,1)S(1)} copy(bf16[1,8,128,1280]{3,2,1,0:T(8,128)(2,1)} %bitcast.16) | data formatting | bytes 5242880
  123.8 2.3 %fusion = f32[3,163840]{1,0:T(4,128)} fusion(bf16[8,163840]{1,0:T(8,128)(2,1)S(1)} %bitcast.37, s32[8]{0:T(128)S(1)} %add_bitcast_fusion, pred[8]{0:T(512)(128)(4,1)S(1)} %compare_reduce_fusion), kind=kOutput, calls=%fused_computation.2 | convolution fusion | flops 8847408 | bytes 4587560 | tf_op jit(solution)/shard_map/dot_general | solution.py:85
  126.1 4.6 %reshape.179 = f32[384,1280]{1,0:T(8,128)} reshape(f32[3,163840]{1,0:T(4,128)} %fusion) | data formatting | bytes 3932160 | tf_op jit(solution)/shard_map/convert_element_type | solution.py:43
  130.6 1.7 reduce_sum.65
  132.4 1.9 multiply_reduce_fusion
  134.3 39.2 %all-gather.4.cloned.1.call-done = bf16[5120,2560]{1,0:T(8,128)(2,1)} async-done(((bf16[320,2560]{1,0:T(8,128)(2,1)}), bf16[5120,2560]{1,0:T(8,128)(2,1)}) %all-gather.4.cloned.1.call-update) | async-done | bytes 26214416 | tf_op jit(solution)/shard_map/all_gather | solution.py:13
  173.5 20.8 %fusion.16 = bf16[384,1280]{1,0:T(8,128)(2,1)S(1)} fusion(f32[384,1280]{1,0:T(8,128)} %reshape.179, bf16[5120,2560]{1,0:T(8,128)(2,1)} %all-gather.4.cloned.1.call-done, f32[1280]{0:T(1024)S(1)} %copy-done.8, f32[384]{0:T(512)S(1)} %add_rsqrt_fusion, f32[384]{0:T(512)S(1)} %broadcast_multiply_fusion), kind=kOutput, calls=%fused_computation.11 | convolution fusion | flops 10081075200 | bytes 31137792 | tf_op jit(solution)/shard_map/dot_general | solution.py:51
  194.3 1.1 broadcast_select_fusion
  (44 shorter events, 1.2 us)
Async XLA Ops:
  7.2 20.1 %copy-start = (bf16[4,4,512,128]{3,2,1,0:T(8,128)(2,1)S(1)}, bf16[4,4,512,128]{3,2,1,0:T(8,128)(2,1)}, u32[]{:S(2)}) copy-start(bf16[4,4,512,128]{3,2,1,0:T(8,128)(2,1)} %param.20) | copy-start | bytes 6291460
  7.2 3.0 %copy-start.7 = (s32[4]{0:T(128)S(1)}, s32[4]{0:T(128)}, u32[]{:S(2)}) copy-start(s32[4]{0:T(128)} %param.14) | copy-start | bytes 52
  7.2 3.0 %copy-start.4 = (s32[4]{0:T(128)S(1)}, s32[4]{0:T(128)}, u32[]{:S(2)}) copy-start(s32[4]{0:T(128)} %param.15) | copy-start | bytes 52
  7.2 166.3 %all-gather.4.cloned.1.call-start = ((), (), s32[]{:S(2)}) async-start(), calls=%async_computation.3 | async-start | bytes 27852800 | tf_op jit(solution)/shard_map/all_gather | solution.py:13
  10.1 17.0 %copy-start.6 = (s32[4]{0:T(128)S(1)}, s32[4]{0:T(128)}, u32[]{:S(2)}) copy-start(s32[4]{0:T(128)} %param.24) | copy-start | bytes 52
  10.1 17.0 %copy-start.2 = (bf16[4,32,128]{2,1,0:T(8,128)(2,1)S(1)}, bf16[4,32,128]{2,1,0:T(8,128)(2,1)}, u32[]{:S(2)}) copy-start(bf16[4,32,128]{2,1,0:T(8,128)(2,1)} %param.19) | copy-start | bytes 98308
  10.1 17.0 %copy-start.9 = (bf16[4,4,128]{2,1,0:T(4,128)(2,1)S(1)}, bf16[4,4,128]{2,1,0:T(4,128)(2,1)}, u32[]{:S(2)}) copy-start(bf16[4,4,128]{2,1,0:T(4,128)(2,1)} %param.22) | copy-start | bytes 12292
  10.2 16.8 %copy-start.5 = (pred[4]{0:T(512)(128)(4,1)}, pred[4]{0:T(512)(128)(4,1)S(1)}, u32[]{:S(2)}) copy-start(pred[4]{0:T(512)(128)(4,1)S(1)} %broadcast_compare_fusion.1) | copy-start | bytes 16
  11.0 20.2 %all-to-all-start = ((bf16[8,1,1]{2,1,0:T(2,128)(2,1)}), bf16[8,1,1]{2,1,0:T(2,128)(2,1)S(1)}, u32[]{:S(2)}, u32[]{:S(2)}) async-start(bf16[8,1,1]{2,1,0:T(2,128)(2,1)} %copy.21), calls=%async_computation | async-start | bytes 8192 | tf_op jit(solution)/shard_map/all_to_all | solution.py:77
  31.2 21.8 %all-to-all-start.2 = ((f32[16,1,128]{2,1,0:T(1,128)}), f32[16,1,128]{2,1,0:T(1,128)S(1)}, u32[]{:S(2)}, u32[]{:S(2)}) async-start(f32[16,1,128]{2,1,0:T(1,128)} %reshape.189), calls=%async_computation.2 | async-start | bytes 16384 | tf_op jit(solution)/shard_map/all_to_all | solution.py:25
  49.6 8.0 %copy-start.3 = (bf16[4,4,128]{2,1,0:T(4,128)(2,1)S(1)}, bf16[4,4,128]{2,1,0:T(4,128)(2,1)}, u32[]{:S(2)}) copy-start(bf16[4,4,128]{2,1,0:T(4,128)(2,1)} %param.23) | copy-start | bytes 12292
  49.6 10.5 %copy-start.1 = (f32[4,4,8,512]{3,2,1,0:T(8,128)S(1)}, f32[4,4,8,512]{3,2,1,0:T(8,128)}, u32[]{:S(2)}) copy-start(f32[4,4,8,512]{3,2,1,0:T(8,128)} %get-tuple-element.5) | copy-start | bytes 786436
  53.0 67.6 %all-to-all-start.1 = ((bf16[8,128,1280]{2,1,0:T(8,128)(2,1)}), bf16[8,128,1280]{2,1,0:T(8,128)(2,1)}, u32[]{:S(2)}, u32[]{:S(2)}) async-start(bf16[8,128,1280]{2,1,0:T(8,128)(2,1)} %copy.22), calls=%async_computation.1 | async-start | bytes 5242880 | tf_op jit(solution)/shard_map/all_to_all | solution.py:76
  130.6 42.9 %copy-start.8 = (f32[1280]{0:T(1024)S(1)}, f32[1280]{0:T(1024)}, u32[]{:S(2)}) copy-start(f32[1280]{0:T(1024)} %param.16) | copy-start | bytes 15364
Sparse Core Ops, SparseCore 0:
  10.3 163.1 all-gather.3
where the time goes:
time: 203 us; the launch traced here: 202 us
  waiting for transfers between devices  62 us (31%)
  blocking collectives  36.8 us (18%)
  starting transfers between devices  32.8 us (16%)
  matrix products  32.2 us (16%)
  local copies, waits for them, and re-layouts  14.3 us (7%)
  between operations  14.3 us (7%)
  other arithmetic  9.94 us (5%)
    all_gather x1, waiting for transfers between devices, gather_turned(): whole = lax.all_gather(both, axis, axis=0, tiled=True)  39.2 us
    all_gather x2, blocking collectives, over_pieces(): blocks = lax.all_gather(array, axis).astype(jnp.float32)  36.8 us
    dot_general x1, matrix products, vit_block(): branch = jnp.dot(hidden, down_whole, preferred_element_type=jnp.float32)  20.8 us
    all_to_all x1, waiting for transfers between devices, place_images(): lax.all_to_all(outgoing, 'dp', split_axis=0, concat_axis=0, tiled=True)  17.7 us
    all_to_all x1, starting transfers between devices, from_everyone(): return lax.all_to_all(copies, axis, split_axis=0, concat_axis=0, tiled=True)  14.4 us
    all_to_all x1, starting transfers between devices, place_images(): lax.all_to_all(sent_counts, 'dp', split_axis=0, concat_axis=0, tiled=True)  13.7 us
    unnamed x24, local copies, waits for them, and re-layouts  6.52 us
    all_to_all x1, starting transfers between devices, place_images(): lax.all_to_all(outgoing, 'dp', split_axis=0, concat_axis=0, tiled=True)  4.58 us
  transfers between devices with their start and end apart: 4, of which 4 were waited for; matrix products, arithmetic and copies ran while one was open for 16% of the time, Pallas kernels for 0%

commit v1 on v0

--- a/solution.py
+++ b/solution.py
@@ -10,7 +10,15 @@
     turned = [jnp.moveaxis(a, dim, 0) for a, dim in zip(arrays, dims)]
     widths = [t[0].size for t in turned]
     both = jnp.concatenate([t.reshape(-1, w) for t, w in zip(turned, widths)], axis=1)
-    whole = lax.all_gather(both, axis, axis=0, tiled=True)
+    whole = jnp.concatenate(
+        lax.all_to_all(
+            jnp.stack([both for _ in range(lax.axis_size(axis))]),
+            axis_name=axis,
+            split_axis=0,
+            concat_axis=0,
+        ),
+        0,
+    )
     blocks = jnp.split(whole, [sum(widths[:k]) for k in range(1, len(widths))], axis=1)
     return tuple(
         (

time: 203 us -> 760 us (3.74)
  blocking collectives: 36.8 us -> 591 us
  between operations: 14.3 us -> 0.86 us
  local copies, waits for them, and re-layouts: 14.3 us -> 22.7 us
    all_gather x2, blocking collectives: 36.8 us -> 591 us  [over_pieces(): blocks = lax.all_gather(array, axis).astype(jnp.float32)]
    all_to_all x1, waiting for transfers between devices: 17.7 us -> 61.7 us  [place_images(): lax.all_to_all(outgoing, 'dp', split_axis=0, concat_axis=0, tiled=True)]
    all_gather x1 -> x0, waiting for transfers between devices: 39.2 us -> none  [gather_turned(): whole = lax.all_gather(both, axis, axis=0, tiled=True)]
    another operation x0 -> x1, local copies, waits for them, and re-layouts: none -> 8.71 us  [gather_turned(): jnp.stack([both for _ in range(lax.axis_size(axis))])]
  transfers between devices with their start and end apart: 4 -> 4, of which waited for: 4 -> 3; matrix products, arithmetic and copies ran while one was open for 16% -> 4% of each run, Pallas kernels for 0% -> 0%
where the time goes in v1:
time: 760 us; the launch traced here: 759 us
  blocking collectives  591 us (78%)
  waiting for transfers between devices  67.2 us (9%)
  starting transfers between devices  38.6 us (5%)
  matrix products  31.6 us (4%)
  local copies, waits for them, and re-layouts  22.7 us (3%)
    all_gather x2, blocking collectives, over_pieces(): blocks = lax.all_gather(array, axis).astype(jnp.float32)  591 us
    all_to_all x1, waiting for transfers between devices, place_images(): lax.all_to_all(outgoing, 'dp', split_axis=0, concat_axis=0, tiled=True)  61.7 us
    dot_general x1, matrix products, vit_block(): branch = jnp.dot(hidden, down_whole, preferred_element_type=jnp.float32)  20.8 us
  transfers between devices with their start and end apart: 4, of which 3 were waited for; matrix products, arithmetic and copies ran while one was open for 4% of the time, Pallas kernels for 0%

profile of v1, /device:TPU:513, one launch (start us, length us, event | category | flops | bytes accessed | tf_op | source)
XLA Modules:
  0.0 759.0 jit_solution(15201431820080480750)
XLA Ops:
  0.7 0.8 broadcast_compare_fusion.1
  1.5 0.8 select_reduce_fusion.1
  2.2 0.7 copy.21
  2.9 13.7 %all-to-all-start = ((bf16[8,1,1]{2,1,0:T(2,128)(2,1)}), bf16[8,1,1]{2,1,0:T(2,128)(2,1)S(1)}, u32[]{:S(2)}, u32[]{:S(2)}) async-start(bf16[8,1,1]{2,1,0:T(2,128)(2,1)} %copy.21), calls=%async_computation | async-start | bytes 8192 | tf_op jit(solution)/shard_map/all_to_all | solution.py:85
  16.6 2.3 copy.27
  19.2 1.4 fusion.52
  20.6 0.8 reshape.195
  21.4 1.7 all-to-all-done
  23.1 14.4 %all-to-all-start.3 = ((f32[16,1,128]{2,1,0:T(1,128)}), f32[16,1,128]{2,1,0:T(1,128)S(1)}, u32[]{:S(2)}, u32[]{:S(2)}) async-start(f32[16,1,128]{2,1,0:T(1,128)} %reshape.195), calls=%async_computation.3 | async-start | bytes 16384 | tf_op jit(solution)/shard_map/all_to_all | solution.py:33
  37.5 1.4 convolution_convert_fusion
  38.9 2.0 copy.22
  40.9 3.8 all-to-all-done.3
  44.6 4.6 all-to-all-start.1
  49.2 1.3 pad_maximum_fusion
  50.5 61.7 %all-to-all-done.1 = bf16[8,128,1280]{2,1,0:T(8,128)(2,1)} async-done(((bf16[8,128,1280]{2,1,0:T(8,128)(2,1)}), bf16[8,128,1280]{2,1,0:T(8,128)(2,1)}, u32[]{:S(2)}, u32[]{:S(2)}) %all-to-all-start.1) | async-done | bytes 2621472 | tf_op jit(solution)/shard_map/all_to_all | solution.py:84
  112.2 8.7 %stack.2 = bf16[16,320,2560]{2,1,0:T(8,128)(2,1)} broadcast(bf16[320,2560]{1,0:T(8,128)(2,1)S(1)} %pad_maximum_fusion), dimensions={1,2} | broadcast | bytes 27852800 | tf_op jit(solution)/shard_map/stack | solution.py:15
  120.9 6.0 all-to-all-start.2
  126.9 0.2 fusion.39
  127.5 0.2 compare_reduce_fusion
  128.0 0.5 broadcast.124
  128.5 0.7 reduce.6
  129.6 574.8 %all-gather.1 = bf16[64,4,8]{2,1,0:T(4,128)(2,1)S(1)} all-gather(bf16[4,4,8]{2,1,0:T(4,128)(2,1)S(1)} %fusion.28), channel_id=3, replica_groups=mesh['group'=2,'tp'=16,'dp'=8] {'tp'}, dimensions={0}, use_global_device_ids=true | all-gather | bytes 4352 | tf_op jit(solution)/shard_map/all_gather | solution.py:42
  704.5 2.0 convolution_convert_fusion.2
  706.5 16.4 %all-gather = bf16[64,4,8,128]{3,2,1,0:T(8,128)(2,1)S(1)} all-gather(bf16[4,4,8,128]{3,2,1,0:T(8,128)(2,1)S(1)} %convolution_convert_fusion.2), channel_id=2, replica_groups=mesh['group'=2,'tp'=16,'dp'=8] {'tp'}, dimensions={0}, use_global_device_ids=true | all-gather | bytes 557056 | tf_op jit(solution)/shard_map/all_gather | solution.py:42
  723.1 3.4 convolution_convert_fusion.3
  726.6 3.2 copy.28
  729.7 2.4 fusion
  732.1 3.2 reshape.185
  735.5 1.1 copy-done.2
  736.6 0.3 multiply_reduce_fusion
  737.0 20.8 %fusion.16 = bf16[384,1280]{1,0:T(8,128)(2,1)S(1)} fusion(f32[384,1280]{1,0:T(8,128)} %copy-done.2, bf16[5120,2560]{1,0:T(8,128)(2,1)} %bitcast.4, f32[1280]{0:T(1024)S(1)} %copy-done.9, f32[384]{0:T(512)S(1)} %add_rsqrt_fusion, f32[384]{0:T(512)S(1)} %broadcast_multiply_fusion), kind=kOutput, calls=%fused_computation.11 | convolution fusion | flops 10081075200 | bytes 31137792 | tf_op jit(solution)/shard_map/dot_general | solution.py:59
  757.9 1.1 broadcast_select_fusion
  (46 shorter events, 1.7 us)
Async XLA Ops:
  0.6 18.6 %copy-start = (bf16[4,4,512,128]{3,2,1,0:T(8,128)(2,1)S(1)}, bf16[4,4,512,128]{3,2,1,0:T(8,128)(2,1)}, u32[]{:S(2)}) copy-start(bf16[4,4,512,128]{3,2,1,0:T(8,128)(2,1)} %param.20) | copy-start | bytes 6291460
  0.6 18.4 %copy-start.8 = (s32[4]{0:T(128)S(1)}, s32[4]{0:T(128)}, u32[]{:S(2)}) copy-start(s32[4]{0:T(128)} %param.24) | copy-start | bytes 52
  0.7 18.4 %copy-start.5 = (bf16[4,32,128]{2,1,0:T(8,128)(2,1)S(1)}, bf16[4,32,128]{2,1,0:T(8,128)(2,1)}, u32[]{:S(2)}) copy-start(bf16[4,32,128]{2,1,0:T(8,128)(2,1)} %param.19) | copy-start | bytes 98308
  0.7 18.4 %copy-start.10 = (bf16[4,4,128]{2,1,0:T(4,128)(2,1)S(1)}, bf16[4,4,128]{2,1,0:T(4,128)(2,1)}, u32[]{:S(2)}) copy-start(bf16[4,4,128]{2,1,0:T(4,128)(2,1)} %param.22) | copy-start | bytes 12292
  2.9 20.2 %all-to-all-start = ((bf16[8,1,1]{2,1,0:T(2,128)(2,1)}), bf16[8,1,1]{2,1,0:T(2,128)(2,1)S(1)}, u32[]{:S(2)}, u32[]{:S(2)}) async-start(bf16[8,1,1]{2,1,0:T(2,128)(2,1)} %copy.21), calls=%async_computation | async-start | bytes 8192 | tf_op jit(solution)/shard_map/all_to_all | solution.py:85
  16.6 20.8 %copy-start.7 = (s32[4]{0:T(128)S(1)}, s32[4]{0:T(128)}, u32[]{:S(2)}) copy-start(s32[4]{0:T(128)} %param.15) | copy-start | bytes 52
  23.1 21.5 %all-to-all-start.3 = ((f32[16,1,128]{2,1,0:T(1,128)}), f32[16,1,128]{2,1,0:T(1,128)S(1)}, u32[]{:S(2)}, u32[]{:S(2)}) async-start(f32[16,1,128]{2,1,0:T(1,128)} %reshape.195), calls=%async_computation.3 | async-start | bytes 16384 | tf_op jit(solution)/shard_map/all_to_all | solution.py:33
  40.8 8.4 %copy-start.4 = (bf16[320,1280]{1,0:T(8,128)(2,1)S(1)}, bf16[320,1280]{1,0:T(8,128)(2,1)}, u32[]{:S(2)}) copy-start(bf16[320,1280]{1,0:T(8,128)(2,1)} %param.18) | copy-start | bytes 2457604
  44.6 67.6 %all-to-all-start.1 = ((bf16[8,128,1280]{2,1,0:T(8,128)(2,1)}), bf16[8,128,1280]{2,1,0:T(8,128)(2,1)}, u32[]{:S(2)}, u32[]{:S(2)}) async-start(bf16[8,128,1280]{2,1,0:T(8,128)(2,1)} %copy.22), calls=%async_computation.1 | async-start | bytes 5242880 | tf_op jit(solution)/shard_map/all_to_all | solution.py:84
  120.9 6.0 copy-start.6
  120.9 8.5 %copy-start.3 = (f32[4,4,8,512]{3,2,1,0:T(8,128)S(1)}, f32[4,4,8,512]{3,2,1,0:T(8,128)}, u32[]{:S(2)}) copy-start(f32[4,4,8,512]{3,2,1,0:T(8,128)} %get-tuple-element.5) | copy-start | bytes 786436
  120.9 616.1 %all-to-all-start.2 = ((bf16[16,320,2560]{2,1,0:T(8,128)(2,1)}), bf16[16,320,2560]{2,1,0:T(8,128)(2,1)}, u32[]{:S(2)}, u32[]{:S(2)}) async-start(bf16[16,320,2560]{2,1,0:T(8,128)(2,1)} %stack.2), calls=%async_computation.2 | async-start | bytes 52428800 | tf_op jit(solution)/shard_map/all_to_all | solution.py:14
  735.3 1.3 copy-start.2
  735.3 1.7 copy-start.9
  737.0 21.9 %copy-start.1 = (bf16[4,4,512,128]{3,2,1,0:T(8,128)(2,1)S(1)}, bf16[4,4,512,128]{3,2,1,0:T(8,128)(2,1)}, u32[]{:S(2)}) copy-start(bf16[4,4,512,128]{3,2,1,0:T(8,128)(2,1)} %param.20) | copy-start | bytes 6291460
